TPU v7x, 32 devices: a whole 2x2x4 slice. The times are simulated.
32 devices in a mesh: wide: 8 (over y, x, core), narrow: 4 (over z).
Axes of the slice: x: 2, y: 2, z: 4, core: 2. Of those that a mesh axis runs over, the one named last changes fastest.
Arguments:
- student_feats: bfloat16 [64, 512], P(('wide', 'narrow')), may hold values from -8 to 8
- teacher_feats: bfloat16 [64, 512], P(('wide', 'narrow')), may hold values from -8 to 8
- prototypes: bfloat16 [16384, 512], P(('wide', 'narrow')), may hold values from -8 to 8
Outputs:
- student_grad: float32 [64, 512], P(('wide', 'narrow'))
- proto_grad: float32 [16384, 512], P(('wide', 'narrow'))
All inputs are finite; a program needn't handle non-finite values.
Results may differ from a plain program's by a relative error of at most 0.0006.
The roundings to bfloat16 on the way count: a program that leaves them out, or rounds other values in their place, can miss the bound.
Values may be sent and summed in bfloat16 or wider, within the bound.
No kernel may reach another device: no remote copies, remote signals or barrier semaphores. Data moves between devices by JAX's collectives and lax.ppermute only.
A program may use at most 64 MiB of HBM per device.

v0:
```python
import jax
import jax.numpy as jnp
from jax import lax
from jax.sharding import PartitionSpec as P

SINK_ITERS = 3


epsilon = 1e-06
teacher_temp = 0.07
student_temp = 0.1
loss_scale = 1.0


def unit_rows(values):
    widened = values.astype(jnp.float32)
    inverse = lax.rsqrt(jnp.sum(widened * widened, axis=1, keepdims=True) + epsilon)
    return (widened * inverse, inverse)


def row_mass(partial_value):
    return lax.psum(partial_value, ("wide", "narrow"))


def on_device(student_feats, teacher_feats, prototypes):
    student_unit, student_inv = unit_rows(student_feats)
    teacher_unit = unit_rows(teacher_feats)[0]
    proto_unit, proto_inv = unit_rows(prototypes)
    proto_hat = proto_unit.astype(jnp.bfloat16)
    paired = jnp.stack([student_unit, teacher_unit]).astype(jnp.bfloat16)
    gathered = lax.all_gather(paired, ("wide", "narrow"), axis=1, tiled=True)
    logits = jnp.einsum("srd,pd->srp", gathered, proto_hat, preferred_element_type=jnp.float32)
    exp_student = jnp.exp(logits[0] / student_temp)
    exp_teacher = jnp.exp(logits[1] / teacher_temp)
    student_part = jnp.sum(exp_student, axis=1)
    col_scale = 1.0 / jnp.sum(exp_teacher, axis=0)
    teacher_part = jnp.sum(exp_teacher * col_scale[None, :], axis=1)
    teacher_total = lax.psum(teacher_part, ("wide", "narrow"))
    row_scale = 1.0 / teacher_total
    for sweep in range(SINK_ITERS - 1):
        col_scale = 1.0 / jnp.sum(exp_teacher * row_scale[:, None], axis=0)
        row_scale = 1.0 / row_mass(jnp.sum(exp_teacher * col_scale[None, :], axis=1))
    student_total = lax.psum(student_part, ("wide", "narrow"))
    target = row_scale[:, None] * exp_teacher * col_scale[None, :]
    student_prob = exp_student / student_total[:, None]
    grad_logits = (loss_scale * (student_prob - target) / student_temp).astype(jnp.bfloat16)
    proto_step = jnp.einsum(
        "bp,bd->pd", grad_logits, gathered[0], preferred_element_type=jnp.float32
    )
    proto_grad = (
        proto_step - proto_unit * jnp.sum(proto_unit * proto_step, axis=1, keepdims=True)
    ) * proto_inv
    outer = lax.psum_scatter(
        jnp.einsum("bp,pd->bd", grad_logits, proto_hat, preferred_element_type=jnp.float32),
        "wide",
        scatter_dimension=0,
        tiled=True,
    )
    row_step = lax.psum_scatter(outer, "narrow", scatter_dimension=0, tiled=True)
    student_grad = (
        row_step - student_unit * jnp.sum(student_unit * row_step, axis=1, keepdims=True)
    ) * student_inv
    return (student_grad, proto_grad)


def solution(mesh):
    placed = (P(("wide", "narrow"), None), P(("wide", "narrow"), None), P(("wide", "narrow"), None))
    return jax.shard_map(
        on_device,
        mesh=mesh,
        in_specs=placed,
        out_specs=(P(("wide", "narrow"), None), P(("wide", "narrow"), None)),
        check_vma=False,
    )
```

profile of v0, /device:TPU:0, one launch (start us, length us, event | category | flops | bytes accessed | tf_op | source)
XLA Modules:
  0.0 261.0 jit_solution(2644794361863399775)
XLA Ops:
  7.2 0.8 fusion.42
  8.0 0.1 fusion.41
  8.2 0.5 copy-done.1
  8.8 70.7 %all_gather.3 = bf16[2,64,512]{2,0,1:T(2,128)(2,1)S(1)} all-gather(bf16[2,2,512]{2,0,1:T(2,128)(2,1)S(1)} %copy.12), channel_id=1, replica_groups=mesh['wide'=8,'narrow'=4] {'wide','narrow'}, dimensions={1}, use_global_device_ids=true | all-gather | bytes 135168 | tf_op jit(solution)/shard_map/all_gather | solution.py:31
  79.5 1.3 copy.13
  80.8 0.2 fusion.6
  81.0 0.3 fusion.7
  81.2 0.1 fusion.23
  81.4 0.1 fusion.14
  81.5 36.9 %psum.29 = f32[64]{0:T(128)S(1)} all-reduce(f32[64]{0:T(128)S(1)} %fusion.14), channel_id=1, replica_groups=mesh['wide'=8,'narrow'=4] {'wide','narrow'}, use_global_device_ids=true, to_apply=%region_7.0 | all-reduce | flops 64 | bytes 512 | tf_op jit(solution)/shard_map/psum | solution.py:38
  118.5 0.1 fusion.16
  118.6 41.3 %psum.30 = f32[64]{0:T(128)S(1)} all-reduce(f32[64]{0:T(128)S(1)} %fusion.16), channel_id=1, replica_groups=mesh['wide'=8,'narrow'=4] {'wide','narrow'}, use_global_device_ids=true, to_apply=%region_10.0 | all-reduce | flops 64 | bytes 512 | tf_op jit(solution)/shard_map/psum | solution.py:22
  160.0 0.1 fusion.18
  160.1 39.4 %all-reduce.1 = (f32[64]{0:T(128)S(1)}, f32[64]{0:T(128)S(1)}) all-reduce(f32[64]{0:T(128)S(1)} %fusion.18, f32[64]{0:T(128)S(1)} %get-tuple-element.8), channel_id=1, replica_groups=mesh['wide'=8,'narrow'=4] {'wide','narrow'}, use_global_device_ids=true, to_apply=%region_13.0 | all-reduce | flops 128 | bytes 1024 | tf_op jit(solution)/shard_map/psum | solution.py:22
  199.5 1.0 fusion.9
  200.5 0.4 fusion.3
  200.9 0.2 fusion.5
  201.2 1.3 copy.17
  202.5 0.7 copy-done.2
  203.1 0.6 dynamic-slice
  204.4 29.6 %reduce-scatter.2.cloned.1.call-done = f32[8,512]{1,0:T(8,128)} async-done(((f32[64,512]{1,0:T(8,128)}), f32[8,512]{1,0:T(8,128)}) %reduce-scatter.2.cloned.1.call-update) | async-done | bytes 16400 | tf_op jit(solution)/shard_map/reduce_scatter | solution.py:53
  234.0 19.4 %all-reduce = f32[8,512]{1,0:T(8,128)S(1)} all-reduce(f32[8,512]{1,0:T(8,128)} %reduce-scatter.2.cloned.1.call-done), channel_id=3, replica_groups=mesh['wide'=8,'narrow'=4] {'narrow'}, use_global_device_ids=true, to_apply=%region_15.0.clone | all-reduce | flops 4096 | bytes 32768
  253.3 0.2 fusion.38
  253.5 0.7 fusion.40
  (21 shorter events, 0.4 us)
Async XLA Ops:
  7.2 0.9 copy-start
  7.2 226.8 %reduce-scatter.2.cloned.1.call-start = ((), (), s32[]{:S(2)}) async-start(), calls=%async_computation.1 | async-start | bytes 147456 | tf_op jit(solution)/shard_map/reduce_scatter | solution.py:53
  8.0 0.7 copy-start.1
  202.5 0.7 copy-start.2
Sparse Core Ops, SparseCore 0:
  200.6 33.2 reduce-scatter.1
where the time goes:
time: 262 us; the launch traced here: 261 us
  blocking collectives  208 us (79%)
  waiting for transfers between devices  29.6 us (11%)
  between operations  14.8 us (6%)
  local copies, waits for them, and re-layouts  4.38 us (2%)
  other arithmetic  2.98 us (1%)
    psum x2, blocking collectives, row_mass(): return lax.psum(partial_value, ('wide', 'narrow'))  80.7 us
    all_gather x1, blocking collectives, on_device(): gathered = lax.all_gather(paired, ('wide', 'narrow'), axis=1, tiled=True)  70.7 us
    psum x1, blocking collectives, on_device(): teacher_total = lax.psum(teacher_part, ('wide', 'narrow'))  36.9 us
    reduce_scatter x1, waiting for transfers between devices, on_device(): lax.psum_scatter(jnp.einsum('bp,pd->bd', grad_logits, proto_hat, preferre...  29.6 us
    unnamed x1, blocking collectives  19.4 us
  transfers between devices with their start and end apart: 1, of which 1 were waited for; matrix products, arithmetic and copies ran while one was open for 1% of the time, Pallas kernels for 0%

commit v1 on v0

v1 whole, which is shorter than its diff:
```python
import jax
import jax.numpy as jnp
from jax import lax
from jax.sharding import PartitionSpec as P

SINK_ITERS = 3
AXES = ("wide", "narrow")

epsilon = 1e-06
teacher_temp = 0.07
student_temp = 0.1
loss_scale = 1.0


def unit_rows(values):
    widened = values.astype(jnp.float32)
    inverse = lax.rsqrt(jnp.sum(widened * widened, axis=1, keepdims=True) + epsilon)
    return (widened * inverse, inverse)


def on_device(devices, student_feats, teacher_feats, prototypes):
    def to_all(block):
        spread = jnp.broadcast_to(block[None], (devices,) + block.shape)
        return lax.all_to_all(spread, AXES, 0, 0, tiled=True)

    def total(partial_value):
        return jnp.sum(to_all(partial_value), axis=0)

    own_rows, width = student_feats.shape
    rows = devices * own_rows
    student_unit, student_inv = unit_rows(student_feats)
    teacher_unit = unit_rows(teacher_feats)[0]
    paired = jnp.stack([student_unit, teacher_unit]).astype(jnp.bfloat16)
    gathered = jnp.swapaxes(to_all(paired), 0, 1).reshape(2, rows, width)
    proto_unit, proto_inv = unit_rows(prototypes)
    proto_hat = proto_unit.astype(jnp.bfloat16)
    logits = jnp.einsum("srd,pd->srp", gathered, proto_hat, preferred_element_type=jnp.float32)
    exp_student = jnp.exp(logits[0] / student_temp)
    exp_teacher = jnp.exp(logits[1] / teacher_temp)
    student_part = jnp.sum(exp_student, axis=1)
    col_scale = 1.0 / jnp.sum(exp_teacher, axis=0)
    for sweep in range(SINK_ITERS - 1):
        row_scale = 1.0 / total(jnp.sum(exp_teacher * col_scale[None, :], axis=1))
        col_scale = 1.0 / jnp.sum(exp_teacher * row_scale[:, None], axis=0)
    teacher_part = jnp.sum(exp_teacher * col_scale[None, :], axis=1)
    totals = total(jnp.stack([teacher_part, student_part]))
    row_scale = 1.0 / totals[0]
    target = row_scale[:, None] * exp_teacher * col_scale[None, :]
    student_prob = exp_student / totals[1][:, None]
    grad_logits = (loss_scale * (student_prob - target) / student_temp).astype(jnp.bfloat16)
    row_part = jnp.einsum("bp,pd->bd", grad_logits, proto_hat, preferred_element_type=jnp.float32)
    row_parts = lax.all_to_all(row_part.reshape(devices, own_rows, width), AXES, 0, 0, tiled=True)
    proto_step = jnp.einsum(
        "bp,bd->pd", grad_logits, gathered[0], preferred_element_type=jnp.float32
    )
    proto_grad = (
        proto_step - proto_unit * jnp.sum(proto_unit * proto_step, axis=1, keepdims=True)
    ) * proto_inv
    row_step = jnp.sum(row_parts, axis=0)
    student_grad = (
        row_step - student_unit * jnp.sum(student_unit * row_step, axis=1, keepdims=True)
    ) * student_inv
    return (student_grad, proto_grad)


def solution(mesh):
    placed = P(AXES, None)
    devices = 1
    for axis in AXES:
        devices *= mesh.shape[axis]

    def body(*args):
        return on_device(devices, *args)

    return jax.shard_map(
        body,
        mesh=mesh,
        in_specs=(placed, placed, placed),
        out_specs=(placed, placed),
        check_vma=False,
    )
```

time: 262 us -> 64.3 us (0.25)
  blocking collectives: 208 us -> 17.8 us
  between operations: 14.8 us -> 0.82 us
  starting transfers between devices: 0.04 us -> 12.4 us
  waiting for transfers between devices: 29.6 us -> 20.3 us
  local copies, waits for them, and re-layouts: 4.38 us -> 7.17 us
    psum x3 -> x0, blocking collectives: 118 us -> none  [the longest x2 80.7 us: row_mass(): return lax.psum(partial_value, ('wide', 'narrow'))]
    all_gather x1 -> x0, blocking collectives: 70.7 us -> none  [on_device(): gathered = lax.all_gather(paired, ('wide', 'narrow'), axis=1, tiled=True)]
    reduce_scatter x1 -> x0, waiting for transfers between devices: 29.6 us -> none  [on_device(): lax.psum_scatter(jnp.einsum('bp,pd->bd', grad_logits, proto_hat, preferre...]
    all_to_all x0 -> x3, waiting for transfers between devices: none -> 20.3 us  [the longest x2 13.8 us: to_all(): return lax.all_to_all(spread, AXES, 0, 0, tiled=True)]
    unnamed x1 -> x0, blocking collectives: 19.4 us -> none
    all_to_all x0 -> x2, blocking collectives: none -> 17.8 us  [to_all(): return lax.all_to_all(spread, AXES, 0, 0, tiled=True)]
    all_to_all x0 -> x3, starting transfers between devices: none -> 12.4 us  [the longest x2 9.87 us: to_all(): return lax.all_to_all(spread, AXES, 0, 0, tiled=True)]
  transfers between devices with their start and end apart: 1 -> 3, of which waited for: 1 -> 3; matrix products, arithmetic and copies ran while one was open for 1% -> 6% of each run, Pallas kernels for 0% -> 0%
where the time goes in v1:
time: 64.3 us; the launch traced here: 64 us
  waiting for transfers between devices  20.3 us (32%)
  blocking collectives  17.8 us (28%)
  starting transfers between devices  12.4 us (19%)
  local copies, waits for them, and re-layouts  7.17 us (11%)
  other arithmetic  4.48 us (7%)
  matrix products  0.96 us (1%)
  between operations  0.82 us (1%)
    all_to_all x2, blocking collectives, to_all(): return lax.all_to_all(spread, AXES, 0, 0, tiled=True)  17.8 us
    all_to_all x2, waiting for transfers between devices, to_all(): return lax.all_to_all(spread, AXES, 0, 0, tiled=True)  13.8 us
    all_to_all x2, starting transfers between devices, to_all(): return lax.all_to_all(spread, AXES, 0, 0, tiled=True)  9.87 us
    all_to_all x1, waiting for transfers between devices, on_device(): lax.all_to_all(row_part.reshape(devices, own_rows, width), AXES, 0, 0, ti...  6.48 us
    unnamed x8, local copies, waits for them, and re-layouts  3.91 us
    all_to_all x1, starting transfers between devices, on_device(): lax.all_to_all(row_part.reshape(devices, own_rows, width), AXES, 0, 0, ti...  2.57 us
  transfers between devices with their start and end apart: 3, of which 3 were waited for; matrix products, arithmetic and copies ran while one was open for 6% of the time, Pallas kernels for 0%

profile of v1, /device:TPU:0, one launch (start us, length us, event | category | flops | bytes accessed | tf_op | source)
XLA Modules:
  0.0 64.0 jit_solution(16009615259203727843)
XLA Ops:
  0.6 0.8 %fusion.40 = f32[2]{0:T(128)S(1)} fusion(bf16[2,512]{1,0:T(2,128)(2,1)} %param.4), kind=kLoop, calls=%fused_computation.53 | loop fusion | flops 3070 | bytes 2056 | tf_op jit(solution)/shard_map/reduce_sum | solution.py:17
  1.6 0.5 copy-done.1
  2.2 0.7 %broadcast_in_dim.8 = bf16[32,2,2,512]{3,2,1,0:T(2,128)(2,1)} broadcast(bf16[2,2,512]{2,1,0:T(2,128)(2,1)S(1)} %pad_maximum_fusion), dimensions={1,2,3} | broadcast | bytes 135168 | tf_op jit(solution)/shard_map/broadcast_in_dim | solution.py:23
  3.0 7.3 %all-to-all-start = ((bf16[32,2,2,512]{3,2,1,0:T(2,128)(2,1)}), bf16[32,2,2,512]{3,2,1,0:T(2,128)(2,1)S(1)}, u32[]{:S(2)}, u32[]{:S(2)}) async-start(bf16[32,2,2,512]{3,2,1,0:T(2,128)(2,1)} %broadcast_in_dim.8), calls=%async_computation | async-start | bytes 262144 | tf_op jit(solution)/shard_map/all_to_all | solution.py:24
  10.3 1.3 %copy.42 = bf16[512,512]{0,1:T(8,128)(2,1)S(1)} copy(bf16[512,512]{1,0:T(8,128)(2,1)} %param.5) | data formatting | bytes 1048576 | tf_op args[2]
  11.7 7.0 %all-to-all-done = bf16[32,2,2,512]{3,2,1,0:T(2,128)(2,1)S(1)} async-done(((bf16[32,2,2,512]{3,2,1,0:T(2,128)(2,1)}), bf16[32,2,2,512]{3,2,1,0:T(2,128)(2,1)S(1)}, u32[]{:S(2)}, u32[]{:S(2)}) %all-to-all-start) | async-done | bytes 131104 | tf_op jit(solution)/shard_map/all_to_all | solution.py:24
  18.8 0.3 fusion.10
  19.4 8.9 %all_to_all.27 = f32[32,1,64]{2,1,0:T(1,128)S(1)} all-to-all(f32[32,1,64]{2,1,0:T(1,128)S(1)} %broadcast_in_dim.9), channel_id=1, replica_groups=mesh['wide'=8,'narrow'=4] {'wide','narrow'}, dimensions={0} | all-to-all | bytes 16384 | tf_op jit(solution)/shard_map/all_to_all | solution.py:24
  28.6 8.9 %all_to_all.28 = f32[32,1,64]{2,1,0:T(1,128)S(1)} all-to-all(f32[32,1,64]{2,1,0:T(1,128)S(1)} %broadcast_in_dim.10), channel_id=1, replica_groups=mesh['wide'=8,'narrow'=4] {'wide','narrow'}, dimensions={0} | all-to-all | bytes 16384 | tf_op jit(solution)/shard_map/all_to_all | solution.py:24
  37.7 0.7 %reshape.155 = f32[32,1,128]{2,1,0:T(1,128)} reshape(f32[32,2,64]{2,1,0:T(2,128)S(1)} %broadcast_in_dim.11) | data formatting | bytes 32768
  38.5 2.5 %all-to-all-start.3 = ((f32[32,1,128]{2,1,0:T(1,128)}), f32[32,1,128]{2,1,0:T(1,128)S(1)}, u32[]{:S(2)}, u32[]{:S(2)}) async-start(f32[32,1,128]{2,1,0:T(1,128)} %reshape.155), calls=%async_computation.3 | async-start | bytes 32768 | tf_op jit(solution)/shard_map/all_to_all | solution.py:24
  41.3 6.9 %all-to-all-done.3 = f32[32,1,128]{2,1,0:T(1,128)S(1)} async-done(((f32[32,1,128]{2,1,0:T(1,128)}), f32[32,1,128]{2,1,0:T(1,128)S(1)}, u32[]{:S(2)}, u32[]{:S(2)}) %all-to-all-start.3) | async-done | bytes 16416 | tf_op jit(solution)/shard_map/all_to_all | solution.py:24
  48.1 0.5 broadcast.143
  48.6 0.7 %reduce.13 = f32[32,128]{1,0:T(8,128)S(1)} reduce(f32[32,1,128]{2,1,0:T(1,128)S(1)} %all-to-all-done.3, f32[]{:T(128)} %broadcast.143), dimensions={1}, to_apply=%all_to_all.20.reduce_sub_computation | reduce | bytes 32772 | tf_op jit(solution)/shard_map/all_to_all | solution.py:24
  49.5 0.5 broadcast.139
  50.0 0.7 %slice_bitcast_fusion = (f32[64]{0:T(128)S(1)}, f32[64]{0:T(128)S(1)}, f32[64]{0:T(128)S(1)}, f32[1,64]{1,0:T(1,128)S(1)}) fusion(f32[2,64]{1,0:T(2,128)S(1)} %reduce_sum.156, f32[]{:T(128)} %broadcast.139), kind=kLoop, calls=%fused_computation.67 | loop fusion | flops 64 | bytes 1540 | tf_op jit(solution)/shard_map/slice | solution.py:49
  51.0 0.3 fusion.8
  51.3 0.7 %copy.52 = f32[32,2,512]{2,1,0:T(2,128)} copy(f32[32,2,512]{2,0,1:T(8,128)S(1)} %fusion.8) | data formatting | bytes 262144 | tf_op jit(solution)/shard_map/bp,pd->bd/dot_general | solution.py:51
  52.1 2.6 %all-to-all-start.4 = ((f32[32,2,512]{2,1,0:T(2,128)}), f32[32,2,512]{2,1,0:T(2,128)S(1)}, u32[]{:S(2)}, u32[]{:S(2)}) async-start(f32[32,2,512]{2,1,0:T(2,128)} %copy.52), calls=%async_computation.4 | async-start | bytes 262144 | tf_op jit(solution)/shard_map/all_to_all | solution.py:52
  54.7 0.4 fusion.3
  55.0 0.2 fusion.5
  55.2 1.3 %copy.53 = f32[512,512]{1,0:T(8,128)} copy(f32[512,512]{0,1:T(8,128)S(1)} %fusion.5) | data formatting | bytes 2097152
  56.6 6.5 %all-to-all-done.4 = f32[32,2,512]{2,1,0:T(2,128)S(1)} async-done(((f32[32,2,512]{2,1,0:T(2,128)}), f32[32,2,512]{2,1,0:T(2,128)S(1)}, u32[]{:S(2)}, u32[]{:S(2)}) %all-to-all-start.4) | async-done | bytes 131104 | tf_op jit(solution)/shard_map/all_to_all | solution.py:52
  63.3 0.7 %fusion.38 = f32[2,512]{1,0:T(2,128)} fusion(f32[2,512]{1,0:T(2,128)S(1)} %reduce_sum.157, bf16[2,512]{1,0:T(2,128)(2,1)S(1)} %copy-done, f32[2]{0:T(128)S(1)} %fusion.36, f32[2]{0:T(128)S(1)} %add_rsqrt_fusion.2), kind=kLoop, calls=%fused_computation.51 | loop fusion | flops 5120 | bytes 10256 | tf_op jit(solution)/shard_map/mul | solution.py:60
  (41 shorter events, 2.3 us)
Async XLA Ops:
  0.6 0.8 %copy-start = (bf16[2,512]{1,0:T(2,128)(2,1)S(1)}, bf16[2,512]{1,0:T(2,128)(2,1)}, u32[]{:S(2)}) copy-start(bf16[2,512]{1,0:T(2,128)(2,1)} %param.3) | copy-start | bytes 6148
  1.5 0.7 %copy-start.1 = (bf16[2,512]{1,0:T(2,128)(2,1)S(1)}, bf16[2,512]{1,0:T(2,128)(2,1)}, u32[]{:S(2)}) copy-start(bf16[2,512]{1,0:T(2,128)(2,1)} %param.4) | copy-start | bytes 6148
  3.0 15.7 %all-to-all-start = ((bf16[32,2,2,512]{3,2,1,0:T(2,128)(2,1)}), bf16[32,2,2,512]{3,2,1,0:T(2,128)(2,1)S(1)}, u32[]{:S(2)}, u32[]{:S(2)}) async-start(bf16[32,2,2,512]{3,2,1,0:T(2,128)(2,1)} %broadcast_in_dim.8), calls=%async_computation | async-start | bytes 262144 | tf_op jit(solution)/shard_map/all_to_all | solution.py:24
  38.5 9.7 %all-to-all-start.3 = ((f32[32,1,128]{2,1,0:T(1,128)}), f32[32,1,128]{2,1,0:T(1,128)S(1)}, u32[]{:S(2)}, u32[]{:S(2)}) async-start(f32[32,1,128]{2,1,0:T(1,128)} %reshape.155), calls=%async_computation.3 | async-start | bytes 32768 | tf_op jit(solution)/shard_map/all_to_all | solution.py:24
  52.1 11.0 %all-to-all-start.4 = ((f32[32,2,512]{2,1,0:T(2,128)}), f32[32,2,512]{2,1,0:T(2,128)S(1)}, u32[]{:S(2)}, u32[]{:S(2)}) async-start(f32[32,2,512]{2,1,0:T(2,128)} %copy.52), calls=%async_computation.4 | async-start | bytes 262144 | tf_op jit(solution)/shard_map/all_to_all | solution.py:52

commit v2 on v1

v2 whole, which is shorter than its diff:
```python
import functools
import math

import jax
import jax.numpy as jnp
from jax import lax
from jax.experimental import pallas as pl
from jax.experimental.pallas import tpu as pltpu
from jax.sharding import PartitionSpec as P

SINK_ITERS = 3
AXES = ("wide", "narrow")
LANES = 128
MIB = 2**20

epsilon = 1e-06
teacher_temp = 0.07
student_temp = 0.1
loss_scale = 1.0

F32 = jnp.float32
BF16 = jnp.bfloat16


def unit_rows(values):
    widened = values.astype(F32)
    inverse = lax.rsqrt(jnp.sum(widened * widened, axis=1, keepdims=True) + epsilon)
    return (widened * inverse, inverse)


def dot(lhs, rhs, lhs_dim, rhs_dim):
    return lax.dot_general(
        lhs, rhs, (((lhs_dim,), (rhs_dim,)), ((), ())), preferred_element_type=F32
    )


def hat_kernel(student_ref, teacher_ref, out_ref):
    devices, both, width = out_ref.shape
    rows = both // 2
    hats = jnp.concatenate(
        [unit_rows(student_ref[...])[0], unit_rows(teacher_ref[...])[0]], axis=0
    ).astype(BF16)
    out_ref[...] = jnp.broadcast_to(hats[None], out_ref.shape)


def first_kernel(hats_ref, protos_ref, teacher_ref, student_ref, hat_ref, part_ref):
    proto_hat = unit_rows(protos_ref[...])[0].astype(BF16)
    hat_ref[...] = proto_hat
    exp_student = jnp.exp(dot(proto_hat, hats_ref[0], 1, 1) / student_temp)
    exp_teacher = jnp.exp(dot(proto_hat, hats_ref[1], 1, 1) / teacher_temp)
    student_ref[...] = exp_student
    teacher_ref[...] = exp_teacher
    col_scale = 1.0 / jnp.sum(exp_teacher, axis=1, keepdims=True)
    part = jnp.concatenate(
        [
            jnp.sum(exp_teacher * col_scale, axis=0, keepdims=True),
            jnp.sum(exp_student, axis=0, keepdims=True),
        ],
        axis=1,
    )
    part_ref[...] = jnp.broadcast_to(part[None], part_ref.shape)


def sweep_kernel(mass_ref, teacher_ref, part_ref):
    rows = teacher_ref.shape[1]
    exp_teacher = teacher_ref[...]
    row_scale = 1.0 / jnp.sum(mass_ref[...], axis=0)[:, :rows]
    col_scale = 1.0 / jnp.sum(exp_teacher * row_scale, axis=1, keepdims=True)
    part = jnp.sum(exp_teacher * col_scale, axis=0, keepdims=True)
    part_ref[...] = jnp.broadcast_to(part[None], part_ref.shape)


def last_sweep_kernel(mass_ref, teacher_ref, part_ref, col_ref):
    rows = teacher_ref.shape[1]
    exp_teacher = teacher_ref[...]
    row_scale = 1.0 / jnp.sum(mass_ref[...], axis=0)[:, :rows]
    col_scale = 1.0 / jnp.sum(exp_teacher * row_scale, axis=1, keepdims=True)
    col_ref[...] = col_scale
    part = jnp.sum(exp_teacher * col_scale, axis=0, keepdims=True)
    part_ref[...] = jnp.broadcast_to(part[None], part_ref.shape)


def grad_kernel(
    first_ref, mass_ref, teacher_ref, student_ref, col_ref, hat_ref, logit_ref, out_ref, step_ref
):
    rows = teacher_ref.shape[1]
    devices = first_ref.shape[0]
    own, width = rows // devices, hat_ref.shape[1]
    student_total = jnp.sum(first_ref[...], axis=0)[:, rows:]
    row_scale = 1.0 / jnp.sum(mass_ref[...], axis=0)
    target = row_scale * teacher_ref[...] * col_ref[...]
    student_prob = student_ref[...] / student_total
    grad_logits = (loss_scale * (student_prob - target) / student_temp).astype(BF16)
    logit_ref[...] = grad_logits
    row_part = dot(grad_logits, hat_ref[...], 0, 0)
    blocks = width // LANES
    for block in range(blocks):
        step_ref[block * rows : (block + 1) * rows, :] = row_part[
            :, block * LANES : (block + 1) * LANES
        ]
    for row in range(own):
        for block in range(blocks):
            out_ref[:, row * blocks + block, :] = step_ref[
                pl.ds(block * rows + row, devices, stride=own), :
            ]


def proto_kernel(logit_ref, hats_ref, protos_ref, out_ref):
    proto_unit, proto_inv = unit_rows(protos_ref[...])
    proto_step = dot(logit_ref[...], hats_ref[0], 1, 0)
    out_ref[...] = (
        proto_step - proto_unit * jnp.sum(proto_unit * proto_step, axis=1, keepdims=True)
    ) * proto_inv


def row_kernel(parts_ref, student_ref, out_ref, step_ref):
    own, width = student_ref.shape
    blocks = width // LANES
    summed = jnp.sum(parts_ref[...], axis=0)
    for row in range(own):
        for block in range(blocks):
            index = row * blocks + block
            step_ref[row : row + 1, block * LANES : (block + 1) * LANES] = summed[index : index + 1]
    row_step = step_ref[...]
    student_unit, student_inv = unit_rows(student_ref[...])
    out_ref[...] = (
        row_step - student_unit * jnp.sum(student_unit * row_step, axis=1, keepdims=True)
    ) * student_inv


def padded_bytes(shape, dtype):
    lanes = -(-shape[-1] // LANES) * LANES
    sublanes = -(-shape[-2] // 8) * 8
    return math.prod(shape[:-2]) * sublanes * lanes * jnp.dtype(dtype).itemsize


def call(kernel, outs, *args, scratch=(), flops=1000):
    vmem = pl.BlockSpec(memory_space=pltpu.VMEM)
    single = not isinstance(outs, (tuple, list))
    shapes = [outs] if single else list(outs)
    sizes = [(shape, dtype) for shape, dtype in shapes] + [(a.shape, a.dtype) for a in args]
    held = sum(padded_bytes(shape, dtype) for shape, dtype in sizes)
    result = pl.pallas_call(
        kernel,
        compiler_params=pltpu.CompilerParams(vmem_limit_bytes=2 * held + 4 * MIB),
        out_shape=[jax.ShapeDtypeStruct(shape, dtype) for shape, dtype in shapes],
        in_specs=[vmem] * len(args),
        out_specs=[vmem] * len(shapes),
        scratch_shapes=list(scratch),
        cost_estimate=pl.CostEstimate(flops=flops, bytes_accessed=0, transcendentals=0),
    )(*args)
    return result[0] if single else result


def on_device(devices, student_feats, teacher_feats, prototypes):
    def exchange(parts):
        return lax.all_to_all(parts, AXES, 0, 0, tiled=True)

    own, width = student_feats.shape
    protos = prototypes.shape[0]
    rows = devices * own
    tiles = own * width // LANES
    hats = exchange(call(hat_kernel, [((devices, 2 * own, width), BF16)], student_feats, teacher_feats)[0])
    hats = hats.reshape(devices, 2, own, width).swapaxes(0, 1).reshape(2, rows, width)
    exp_teacher, exp_student, proto_hat, part = call(
        first_kernel,
        [
            ((protos, rows), F32),
            ((protos, rows), F32),
            ((protos, width), BF16),
            ((devices, 1, 2 * rows), F32),
        ],
        hats,
        prototypes,
    )
    first = mass = exchange(part)
    for sweep in range(SINK_ITERS - 2):
        mass = exchange(call(sweep_kernel, [((devices, 1, rows), F32)], mass, exp_teacher)[0])
    part, col_scale = call(
        last_sweep_kernel, [((devices, 1, rows), F32), ((protos, 1), F32)], mass, exp_teacher
    )
    mass = exchange(part)
    grad_logits, parts = call(
        grad_kernel,
        [((protos, rows), BF16), ((devices, tiles, LANES), F32)],
        first,
        mass,
        exp_teacher,
        exp_student,
        col_scale,
        proto_hat,
        scratch=[pltpu.VMEM((rows * width // LANES, LANES), F32)],
    )
    parts = exchange(parts)
    proto_grad = call(
        proto_kernel, [((protos, width), F32)], grad_logits, hats, prototypes, flops=10**9
    )[0]
    student_grad = call(
        row_kernel,
        [((own, width), F32)],
        parts,
        student_feats,
        scratch=[pltpu.VMEM((own, width), F32)],
    )[0]
    return (student_grad, proto_grad)


def solution(mesh):
    placed = P(AXES, None)
    devices = 1
    for axis in AXES:
        devices *= mesh.shape[axis]
    return jax.shard_map(
        functools.partial(on_device, devices),
        mesh=mesh,
        in_specs=(placed, placed, placed),
        out_specs=(placed, placed),
        check_vma=False,
    )
```

time: 64.3 us -> 58.7 us (0.913)
  blocking collectives: 17.8 us -> 42.2 us
  waiting for transfers between devices: 20.3 us -> 6.97 us
  starting transfers between devices: 12.4 us -> 2.57 us
  local copies, waits for them, and re-layouts: 7.17 us -> 1.58 us
  other arithmetic: 4.48 us -> 0 us
  Pallas kernels: 0 us -> 4.4 us
  matrix products: 0.96 us -> 0 us
    all_to_all x2 -> x4, blocking collectives: 17.8 us -> 42.2 us  [exchange(): return lax.all_to_all(parts, AXES, 0, 0, tiled=True)]
    all_to_all x3 -> x1, waiting for transfers between devices: 20.3 us -> 6.97 us  [exchange(): return lax.all_to_all(parts, AXES, 0, 0, tiled=True)]
    all_to_all x3 -> x1, starting transfers between devices: 12.4 us -> 2.57 us  [exchange(): return lax.all_to_all(parts, AXES, 0, 0, tiled=True)]
    pallas_call x0 -> x7, Pallas kernels: none -> 4.4 us  [call(): pl.pallas_call(kernel, compiler_params=pltpu.CompilerParams(vmem_limit_by...]
    unnamed x8, local copies, waits for them, and re-layouts: 3.91 us -> 1.37 us
    reduce_sum x14 -> x0, other arithmetic: 2.11 us -> none  [the longest x3 1.07 us: unit_rows(): jnp.sum(widened * widened, axis=1, keepdims=True) + epsilon]
    dot_general x3 -> x0, matrix products: 0.96 us -> none  [the longest x1 0.39 us: on_device(): jnp.einsum('bp,bd->pd', grad_logits, gathered[0], preferred_element_type=...]
    mul x2 -> x0, other arithmetic: 0.87 us -> none  [the longest x1 0.67 us: on_device(): (row_step - student_unit * jnp.sum(student_unit * row_step, axis=1, keepd...]
  transfers between devices with their start and end apart: 3 -> 1, of which waited for: 3 -> 1; matrix products, arithmetic and copies ran while one was open for 6% -> 0% of each run, Pallas kernels for 0% -> 2%
where the time goes in v2:
time: 58.7 us; the launch traced here: 58.4 us
  blocking collectives  42.2 us (72%)
  waiting for transfers between devices  6.97 us (12%)
  Pallas kernels  4.4 us (7%)
  starting transfers between devices  2.57 us (4%)
  local copies, waits for them, and re-layouts  1.58 us (3%)
  between operations  0.72 us (1%)
    all_to_all x4, blocking collectives, exchange(): return lax.all_to_all(parts, AXES, 0, 0, tiled=True)  42.2 us
    all_to_all x1, waiting for transfers between devices, exchange(): return lax.all_to_all(parts, AXES, 0, 0, tiled=True)  6.97 us
    pallas_call x7, Pallas kernels, call(): pl.pallas_call(kernel, compiler_params=pltpu.CompilerParams(vmem_limit_by...  4.4 us
    all_to_all x1, starting transfers between devices, exchange(): return lax.all_to_all(parts, AXES, 0, 0, tiled=True)  2.57 us
    unnamed x8, local copies, waits for them, and re-layouts  1.37 us
  transfers between devices with their start and end apart: 1, of which 1 were waited for; matrix products, arithmetic and copies ran while one was open for 0% of the time, Pallas kernels for 2%

profile of v2, /device:TPU:0, one launch (start us, length us, event | category | flops | bytes accessed | tf_op | source)
XLA Modules:
  0.0 58.4 jit_solution(16490880196354726358)
XLA Ops:
  0.6 0.0 copy-start.1
  0.6 0.7 %copy-done.1 = bf16[2,512]{1,0:T(2,128)(2,1)S(1)} copy-done((bf16[2,512]{1,0:T(2,128)(2,1)S(1)}, bf16[2,512]{1,0:T(2,128)(2,1)}, u32[]{:S(2)}) %copy-start.1) | copy-done | bytes 2072
  1.3 0.0 copy-start.3
  1.3 0.7 %copy-done.3 = bf16[2,512]{1,0:T(2,128)(2,1)S(1)} copy-done((bf16[2,512]{1,0:T(2,128)(2,1)S(1)}, bf16[2,512]{1,0:T(2,128)(2,1)}, u32[]{:S(2)}) %copy-start.3) | copy-done | bytes 2072
  2.0 0.1 shard_map.50
  2.1 0.0 copy-start
  2.1 15.5 %all_to_all.25 = bf16[32,4,512]{2,1,0:T(4,128)(2,1)S(1)} all-to-all(bf16[32,4,512]{2,1,0:T(4,128)(2,1)S(1)} %shard_map.50), channel_id=1, replica_groups=mesh['wide'=8,'narrow'=4] {'wide','narrow'}, dimensions={0} | all-to-all | bytes 262144 | tf_op jit(solution)/shard_map/all_to_all | solution.py:157
  17.6 0.1 reshape.10
  17.7 0.1 copy.7
  17.8 0.1 reshape.11.hats_ref
  17.9 0.0 copy-done
  17.9 0.6 %shard_map.51 = (f32[512,64]{1,0:T(8,128)S(1)}, f32[512,64]{1,0:T(8,128)S(1)}, bf16[512,512]{1,0:T(8,128)(2,1)S(1)}, f32[32,1,128]{2,1,0:T(1,128)S(1)}) custom-call(bf16[2,64,512]{2,1,0:T(8,128)(2,1)S(1)} %reshape.11.hats_ref, bf16[512,512]{1,0:T(8,128)(2,1)S(1)} %copy-done), custom_call_target="tpu_custom_call" | custom-call | flops 1000 | tf_op jit(solution)/shard_map/pallas_call | solution.py:143
  18.5 8.9 %all_to_all.26.mass_ref.first_ref = f32[32,1,128]{2,1,0:T(1,128)S(1)} all-to-all(f32[32,1,128]{2,1,0:T(1,128)S(1)} %get-tuple-element.10), channel_id=1, replica_groups=mesh['wide'=8,'narrow'=4] {'wide','narrow'}, dimensions={0} | all-to-all | bytes 32768 | tf_op jit(solution)/shard_map/all_to_all | solution.py:157
  27.4 0.2 shard_map.52
  27.6 8.9 %all_to_all.27.mass_ref = f32[32,1,64]{2,1,0:T(1,128)S(1)} all-to-all(f32[32,1,64]{2,1,0:T(1,128)S(1)} %shard_map.52), channel_id=1, replica_groups=mesh['wide'=8,'narrow'=4] {'wide','narrow'}, dimensions={0} | all-to-all | bytes 16384 | tf_op jit(solution)/shard_map/all_to_all | solution.py:157
  36.5 0.2 shard_map.53
  36.7 8.9 %all_to_all.28.mass_ref = f32[32,1,64]{2,1,0:T(1,128)S(1)} all-to-all(f32[32,1,64]{2,1,0:T(1,128)S(1)} %get-tuple-element.12), channel_id=1, replica_groups=mesh['wide'=8,'narrow'=4] {'wide','narrow'}, dimensions={0} | all-to-all | bytes 16384 | tf_op jit(solution)/shard_map/all_to_all | solution.py:157
  45.6 1.1 %shard_map.54 = (bf16[512,64]{1,0:T(8,128)(2,1)S(1)}, f32[32,8,128]{2,1,0:T(8,128)}) custom-call(f32[32,1,128]{2,1,0:T(1,128)S(1)} %all_to_all.26.mass_ref.first_ref, f32[32,1,64]{2,1,0:T(1,128)S(1)} %all_to_all.28.mass_ref, f32[512,64]{1,0:T(8,128)S(1)} %get-tuple-element.11.teacher_ref, f32[512,64]{1,0:T(8,128)S(1)} %get-tuple-element.13.student_ref, ...), custom_call_target="tpu_custom_call" | custom-call | flops 1000 | tf_op jit(solution)/shard_map/pallas_call | solution.py:143
  46.7 2.6 %all-to-all-start.4 = ((f32[32,8,128]{2,1,0:T(8,128)}), f32[32,8,128]{2,1,0:T(8,128)S(1)}, u32[]{:S(2)}, u32[]{:S(2)}) async-start(f32[32,8,128]{2,1,0:T(8,128)} %get-tuple-element.16), calls=%async_computation.4 | async-start | bytes 262144 | tf_op jit(solution)/shard_map/all_to_all | solution.py:157
  49.3 0.0 copy-start.2
  49.3 1.4 %shard_map.56 = f32[512,512]{1,0:T(8,128)} custom-call(bf16[512,64]{1,0:T(8,128)(2,1)S(1)} %get-tuple-element.17.logit_ref, bf16[2,64,512]{2,1,0:T(8,128)(2,1)S(1)} %reshape.11.hats_ref, bf16[512,512]{1,0:T(8,128)(2,1)S(1)} %copy-done), custom_call_target="tpu_custom_call" | custom-call | flops 1000000000 | tf_op jit(solution)/shard_map/pallas_call | solution.py:143
  50.7 7.0 %all-to-all-done.4.parts_ref = f32[32,8,128]{2,1,0:T(8,128)S(1)} async-done(((f32[32,8,128]{2,1,0:T(8,128)}), f32[32,8,128]{2,1,0:T(8,128)S(1)}, u32[]{:S(2)}, u32[]{:S(2)}) %all-to-all-start.4) | async-done | bytes 131104 | tf_op jit(solution)/shard_map/all_to_all | solution.py:157
  57.6 0.0 copy-done.2
  57.6 0.8 %shard_map.55 = f32[2,512]{1,0:T(2,128)} custom-call(f32[32,8,128]{2,1,0:T(8,128)S(1)} %all-to-all-done.4.parts_ref, bf16[2,512]{1,0:T(2,128)(2,1)S(1)} %copy-done.2), custom_call_target="tpu_custom_call" | custom-call | flops 1000 | tf_op jit(solution)/shard_map/pallas_call | solution.py:143
Async XLA Ops:
  0.6 0.7 %copy-start.1 = (bf16[2,512]{1,0:T(2,128)(2,1)S(1)}, bf16[2,512]{1,0:T(2,128)(2,1)}, u32[]{:S(2)}) copy-start(bf16[2,512]{1,0:T(2,128)(2,1)} %student_ref.3) | copy-start | bytes 6148
  1.3 0.7 %copy-start.3 = (bf16[2,512]{1,0:T(2,128)(2,1)S(1)}, bf16[2,512]{1,0:T(2,128)(2,1)}, u32[]{:S(2)}) copy-start(bf16[2,512]{1,0:T(2,128)(2,1)} %teacher_ref.1) | copy-start | bytes 6148
  2.1 15.7 %copy-start = (bf16[512,512]{1,0:T(8,128)(2,1)S(1)}, bf16[512,512]{1,0:T(8,128)(2,1)}, u32[]{:S(2)}) copy-start(bf16[512,512]{1,0:T(8,128)(2,1)} %protos_ref.3) | copy-start | bytes 1572868
  46.7 11.0 %all-to-all-start.4 = ((f32[32,8,128]{2,1,0:T(8,128)}), f32[32,8,128]{2,1,0:T(8,128)S(1)}, u32[]{:S(2)}, u32[]{:S(2)}) async-start(f32[32,8,128]{2,1,0:T(8,128)} %get-tuple-element.16), calls=%async_computation.4 | async-start | bytes 262144 | tf_op jit(solution)/shard_map/all_to_all | solution.py:157
  49.3 8.4 %copy-start.2 = (bf16[2,512]{1,0:T(2,128)(2,1)S(1)}, bf16[2,512]{1,0:T(2,128)(2,1)}, u32[]{:S(2)}) copy-start(bf16[2,512]{1,0:T(2,128)(2,1)} %student_ref.3) | copy-start | bytes 6148

commit v3 on v2

--- a/solution.py
+++ b/solution.py
@@ -12,6 +12,7 @@
 AXES = ("wide", "narrow")
 LANES = 128
 MIB = 2**20
+CHUNKS = 4
 
 epsilon = 1e-06
 teacher_temp = 0.07
@@ -28,23 +29,57 @@
     return (widened * inverse, inverse)
 
 
+def narrow(values):
+    scaled = values * 65537.0
+    return scaled - (scaled - values)
+
+
+def unit_rows_close(values):
+    widened = values.astype(F32)
+    squares = widened * widened
+    step = 2.0 * jnp.sum(squares, axis=1, keepdims=True)
+    high = (squares + step) - step
+    low = jnp.sum(squares - high, axis=1, keepdims=True) + epsilon
+    high = jnp.sum(high, axis=1, keepdims=True)
+    total = high + low
+    rest = (high - total) + low
+    inverse = lax.rsqrt(total)
+    head = narrow(inverse)
+    tail = inverse - head
+    square = head * head
+    total_head = narrow(total)
+    total_tail = total - total_head
+    total_mid = narrow(total_tail)
+    miss = (1.0 - total_head * square) - total_mid * square
+    miss = miss - (total_tail - total_mid) * square
+    miss = miss - total * (2.0 * head * tail)
+    miss = miss - (total * tail * tail + rest * square)
+    inverse = inverse + 0.5 * inverse * miss
+    return (widened * inverse, inverse)
+
+
 def dot(lhs, rhs, lhs_dim, rhs_dim):
     return lax.dot_general(
         lhs, rhs, (((lhs_dim,), (rhs_dim,)), ((), ())), preferred_element_type=F32
     )
 
 
-def hat_kernel(student_ref, teacher_ref, out_ref):
-    devices, both, width = out_ref.shape
-    rows = both // 2
-    hats = jnp.concatenate(
-        [unit_rows(student_ref[...])[0], unit_rows(teacher_ref[...])[0]], axis=0
-    ).astype(BF16)
-    out_ref[...] = jnp.broadcast_to(hats[None], out_ref.shape)
-
-
-def first_kernel(hats_ref, protos_ref, teacher_ref, student_ref, hat_ref, part_ref):
-    proto_hat = unit_rows(protos_ref[...])[0].astype(BF16)
+def hat_kernel(student_ref, teacher_ref, out_ref, held_ref, sems):
+    copies = [
+        pltpu.make_async_copy(source, held_ref.at[index], sems.at[index])
+        for index, source in enumerate((student_ref, teacher_ref))
+    ]
+    for copy in copies:
+        copy.start()
+    for copy in copies:
+        copy.wait()
+    hats = jnp.concatenate([unit_rows_close(held_ref[index])[0] for index in range(2)], axis=0)
+    out_ref[...] = jnp.broadcast_to(hats.astype(BF16)[None], out_ref.shape)
+
+
+def first_kernel(hats_ref, protos_ref, teacher_ref, student_ref, hat_ref, inv_ref, part_ref):
+    proto_unit, inv_ref[...] = unit_rows_close(protos_ref[...])
+    proto_hat = proto_unit.astype(BF16)
     hat_ref[...] = proto_hat
     exp_student = jnp.exp(dot(proto_hat, hats_ref[0], 1, 1) / student_temp)
     exp_teacher = jnp.exp(dot(proto_hat, hats_ref[1], 1, 1) / teacher_temp)
@@ -81,9 +116,22 @@
 
 
 def grad_kernel(
-    first_ref, mass_ref, teacher_ref, student_ref, col_ref, hat_ref, logit_ref, out_ref, step_ref
+    first_ref,
+    mass_ref,
+    teacher_ref,
+    student_ref,
+    col_ref,
+    hats_ref,
+    hat_ref,
+    protos_ref,
+    inv_ref,
+    out_ref,
+    grad_ref,
+    step_ref,
+    held_ref,
+    sems,
 ):
-    rows = teacher_ref.shape[1]
+    protos, rows = teacher_ref.shape
     devices = first_ref.shape[0]
     own, width = rows // devices, hat_ref.shape[1]
     student_total = jnp.sum(first_ref[...], axis=0)[:, rows:]
@@ -91,7 +139,17 @@
     target = row_scale * teacher_ref[...] * col_ref[...]
     student_prob = student_ref[...] / student_total
     grad_logits = (loss_scale * (student_prob - target) / student_temp).astype(BF16)
-    logit_ref[...] = grad_logits
+    copies = []
+    tall = protos // CHUNKS
+    for chunk in range(CHUNKS):
+        part = slice(chunk * tall, (chunk + 1) * tall)
+        proto_step = dot(grad_logits[part], hats_ref[0], 1, 0)
+        proto_inv = inv_ref[part]
+        proto_unit = protos_ref[part].astype(F32) * proto_inv
+        along = jnp.sum(proto_unit * proto_step, axis=1, keepdims=True)
+        held_ref[part] = (proto_step - proto_unit * along) * proto_inv
+        copies.append(pltpu.make_async_copy(held_ref.at[part], grad_ref.at[part], sems.at[chunk]))
+        copies[-1].start()
     row_part = dot(grad_logits, hat_ref[...], 0, 0)
     blocks = width // LANES
     for block in range(blocks):
@@ -103,14 +161,8 @@
             out_ref[:, row * blocks + block, :] = step_ref[
                 pl.ds(block * rows + row, devices, stride=own), :
             ]
-
-
-def proto_kernel(logit_ref, hats_ref, protos_ref, out_ref):
-    proto_unit, proto_inv = unit_rows(protos_ref[...])
-    proto_step = dot(logit_ref[...], hats_ref[0], 1, 0)
-    out_ref[...] = (
-        proto_step - proto_unit * jnp.sum(proto_unit * proto_step, axis=1, keepdims=True)
-    ) * proto_inv
+    for copy in copies:
+        copy.wait()
 
 
 def row_kernel(parts_ref, student_ref, out_ref, step_ref):
@@ -134,22 +186,20 @@
     return math.prod(shape[:-2]) * sublanes * lanes * jnp.dtype(dtype).itemsize
 
 
-def call(kernel, outs, *args, scratch=(), flops=1000):
-    vmem = pl.BlockSpec(memory_space=pltpu.VMEM)
-    single = not isinstance(outs, (tuple, list))
-    shapes = [outs] if single else list(outs)
-    sizes = [(shape, dtype) for shape, dtype in shapes] + [(a.shape, a.dtype) for a in args]
-    held = sum(padded_bytes(shape, dtype) for shape, dtype in sizes)
-    result = pl.pallas_call(
+def call(kernel, outs, *args, scratch=(), inputs=pltpu.VMEM, far=()):
+    held = sum(padded_bytes(a.shape, a.dtype) for a in args)
+    held += sum(padded_bytes(shape, dtype) for shape, dtype in outs)
+    return pl.pallas_call(
         kernel,
         compiler_params=pltpu.CompilerParams(vmem_limit_bytes=2 * held + 4 * MIB),
-        out_shape=[jax.ShapeDtypeStruct(shape, dtype) for shape, dtype in shapes],
-        in_specs=[vmem] * len(args),
-        out_specs=[vmem] * len(shapes),
+        out_shape=[jax.ShapeDtypeStruct(shape, dtype) for shape, dtype in outs],
+        in_specs=[pl.BlockSpec(memory_space=inputs)] * len(args),
+        out_specs=[
+            pl.BlockSpec(memory_space=pltpu.HBM if index in far else pltpu.VMEM)
+            for index in range(len(outs))
+        ],
         scratch_shapes=list(scratch),
-        cost_estimate=pl.CostEstimate(flops=flops, bytes_accessed=0, transcendentals=0),
     )(*args)
-    return result[0] if single else result
 
 
 def on_device(devices, student_feats, teacher_feats, prototypes):
@@ -160,14 +210,23 @@
     protos = prototypes.shape[0]
     rows = devices * own
     tiles = own * width // LANES
-    hats = exchange(call(hat_kernel, [((devices, 2 * own, width), BF16)], student_feats, teacher_feats)[0])
+    spread = call(
+        hat_kernel,
+        [((devices, 2 * own, width), BF16)],
+        pltpu.with_memory_space_constraint(student_feats, pltpu.HBM),
+        pltpu.with_memory_space_constraint(teacher_feats, pltpu.HBM),
+        scratch=[pltpu.VMEM((2, own, width), BF16), pltpu.SemaphoreType.DMA((2,))],
+        inputs=pltpu.HBM,
+    )[0]
+    hats = exchange(spread)
     hats = hats.reshape(devices, 2, own, width).swapaxes(0, 1).reshape(2, rows, width)
-    exp_teacher, exp_student, proto_hat, part = call(
+    exp_teacher, exp_student, proto_hat, proto_inv, part = call(
         first_kernel,
         [
             ((protos, rows), F32),
             ((protos, rows), F32),
             ((protos, width), BF16),
+            ((protos, 1), F32),
             ((devices, 1, 2 * rows), F32),
         ],
         hats,
@@ -180,25 +239,29 @@
         last_sweep_kernel, [((devices, 1, rows), F32), ((protos, 1), F32)], mass, exp_teacher
     )
     mass = exchange(part)
-    grad_logits, parts = call(
+    parts, proto_grad = call(
         grad_kernel,
-        [((protos, rows), BF16), ((devices, tiles, LANES), F32)],
+        [((devices, tiles, LANES), F32), ((protos, width), F32)],
         first,
         mass,
         exp_teacher,
         exp_student,
         col_scale,
+        hats,
         proto_hat,
-        scratch=[pltpu.VMEM((rows * width // LANES, LANES), F32)],
-    )
-    parts = exchange(parts)
-    proto_grad = call(
-        proto_kernel, [((protos, width), F32)], grad_logits, hats, prototypes, flops=10**9
-    )[0]
+        prototypes,
+        proto_inv,
+        scratch=[
+            pltpu.VMEM((rows * width // LANES, LANES), F32),
+            pltpu.VMEM((protos, width), F32),
+            pltpu.SemaphoreType.DMA((CHUNKS,)),
+        ],
+        far=(1,),
+    )
     student_grad = call(
         row_kernel,
         [((own, width), F32)],
-        parts,
+        exchange(parts),
         student_feats,
         scratch=[pltpu.VMEM((own, width), F32)],
     )[0]

time: 58.7 us -> 58.1 us (0.990)
  blocking collectives: 42.2 us -> 52.3 us
  waiting for transfers between devices: 6.97 us -> 0 us
  starting transfers between devices: 2.57 us -> 0 us
  local copies, waits for them, and re-layouts: 1.58 us -> 0.22 us
    all_to_all x4 -> x5, blocking collectives: 42.2 us -> 52.3 us  [exchange(): return lax.all_to_all(parts, AXES, 0, 0, tiled=True)]
    all_to_all x1 -> x0, waiting for transfers between devices: 6.97 us -> none  [exchange(): return lax.all_to_all(parts, AXES, 0, 0, tiled=True)]
    all_to_all x1 -> x0, starting transfers between devices: 2.57 us -> none  [exchange(): return lax.all_to_all(parts, AXES, 0, 0, tiled=True)]
    unnamed x8 -> x4, local copies, waits for them, and re-layouts: 1.37 us -> 0.01 us
    pallas_call x7 -> x6, Pallas kernels: 4.4 us -> 4.66 us  [call(): pl.pallas_call(kernel, compiler_params=pltpu.CompilerParams(vmem_limit_by...]
  transfers between devices with their start and end apart: 1 -> 0, of which waited for: 1 -> 0; matrix products, arithmetic and copies ran while one was open for 0% -> 0% of each run, Pallas kernels for 2% -> 0%
where the time goes in v3:
time: 58.1 us; the launch traced here: 57.9 us
  blocking collectives  52.3 us (90%)
  Pallas kernels  4.66 us (8%)
  between operations  0.71 us (1%)
    all_to_all x5, blocking collectives, exchange(): return lax.all_to_all(parts, AXES, 0, 0, tiled=True)  52.3 us
    pallas_call x6, Pallas kernels, call(): pl.pallas_call(kernel, compiler_params=pltpu.CompilerParams(vmem_limit_by...  4.66 us

profile of v3, /device:TPU:0, one launch (start us, length us, event | category | flops | bytes accessed | tf_op | source)
XLA Modules:
  0.0 57.9 jit_solution(13122761510819228403)
XLA Ops:
  0.6 0.9 %shard_map.50 = bf16[32,4,512]{2,1,0:T(4,128)(2,1)S(1)} custom-call(bf16[2,512]{1,0:T(2,128)(2,1)} %student_ref.3, bf16[2,512]{1,0:T(2,128)(2,1)} %teacher_ref.1), custom_call_target="tpu_custom_call" | custom-call | tf_op jit(solution)/shard_map/pallas_call | solution.py:192
  1.6 0.0 copy-start
  1.6 15.5 %all_to_all.25 = bf16[32,4,512]{2,1,0:T(4,128)(2,1)S(1)} all-to-all(bf16[32,4,512]{2,1,0:T(4,128)(2,1)S(1)} %shard_map.50), channel_id=1, replica_groups=mesh['wide'=8,'narrow'=4] {'wide','narrow'}, dimensions={0} | all-to-all | bytes 262144 | tf_op jit(solution)/shard_map/all_to_all | solution.py:207
  17.1 0.1 reshape.10
  17.1 0.1 copy.7
  17.2 0.1 reshape.11.hats_ref
  17.3 0.0 copy-done
  17.3 1.1 %shard_map.51 = (f32[512,64]{1,0:T(8,128)S(1)}, f32[512,64]{1,0:T(8,128)S(1)}, bf16[512,512]{1,0:T(8,128)(2,1)S(1)}, f32[512,1]{1,0:T(8,128)S(1)}, f32[32,1,128]{2,1,0:T(1,128)S(1)}) custom-call(bf16[2,64,512]{2,1,0:T(8,128)(2,1)S(1)} %reshape.11.hats_ref, bf16[512,512]{1,0:T(8,128)(2,1)S(1)} %copy-done), custom_call_target="tpu_custom_call" | custom-call | tf_op jit(solution)/shard_map/pallas_call | solution.py:192
  18.4 8.9 %all_to_all.26.mass_ref.first_ref = f32[32,1,128]{2,1,0:T(1,128)S(1)} all-to-all(f32[32,1,128]{2,1,0:T(1,128)S(1)} %get-tuple-element.11), channel_id=1, replica_groups=mesh['wide'=8,'narrow'=4] {'wide','narrow'}, dimensions={0} | all-to-all | bytes 32768 | tf_op jit(solution)/shard_map/all_to_all | solution.py:207
  27.3 0.2 shard_map.52
  27.5 8.9 %all_to_all.27.mass_ref = f32[32,1,64]{2,1,0:T(1,128)S(1)} all-to-all(f32[32,1,64]{2,1,0:T(1,128)S(1)} %shard_map.52), channel_id=1, replica_groups=mesh['wide'=8,'narrow'=4] {'wide','narrow'}, dimensions={0} | all-to-all | bytes 16384 | tf_op jit(solution)/shard_map/all_to_all | solution.py:207
  36.4 0.2 shard_map.53
  36.6 8.9 %all_to_all.28.mass_ref = f32[32,1,64]{2,1,0:T(1,128)S(1)} all-to-all(f32[32,1,64]{2,1,0:T(1,128)S(1)} %get-tuple-element.13), channel_id=1, replica_groups=mesh['wide'=8,'narrow'=4] {'wide','narrow'}, dimensions={0} | all-to-all | bytes 16384 | tf_op jit(solution)/shard_map/all_to_all | solution.py:207
  45.5 1.5 %shard_map.54 = (f32[32,8,128]{2,1,0:T(8,128)S(1)}, f32[512,512]{1,0:T(8,128)}) custom-call(f32[32,1,128]{2,1,0:T(1,128)S(1)} %all_to_all.26.mass_ref.first_ref, f32[32,1,64]{2,1,0:T(1,128)S(1)} %all_to_all.28.mass_ref, f32[512,64]{1,0:T(8,128)S(1)} %get-tuple-element.12.teacher_ref, f32[512,64]{1,0:T(8,128)S(1)} %get-tuple-element.14.student_ref, ...), custom_call_target="tpu_custom_call" | custom-call | tf_op jit(solution)/shard_map/pallas_call | solution.py:192
  47.0 0.0 copy-start.1
  47.0 10.1 %all_to_all.29.parts_ref = f32[32,8,128]{2,1,0:T(8,128)S(1)} all-to-all(f32[32,8,128]{2,1,0:T(8,128)S(1)} %get-tuple-element.18), channel_id=1, replica_groups=mesh['wide'=8,'narrow'=4] {'wide','narrow'}, dimensions={0} | all-to-all | bytes 262144 | tf_op jit(solution)/shard_map/all_to_all | solution.py:207
  57.1 0.0 copy-done.1
  57.1 0.8 %shard_map.55 = f32[2,512]{1,0:T(2,128)} custom-call(f32[32,8,128]{2,1,0:T(8,128)S(1)} %all_to_all.29.parts_ref, bf16[2,512]{1,0:T(2,128)(2,1)S(1)} %copy-done.1), custom_call_target="tpu_custom_call" | custom-call | tf_op jit(solution)/shard_map/pallas_call | solution.py:192
Async XLA Ops:
  1.6 15.7 %copy-start = (bf16[512,512]{1,0:T(8,128)(2,1)S(1)}, bf16[512,512]{1,0:T(8,128)(2,1)}, u32[]{:S(2)}) copy-start(bf16[512,512]{1,0:T(8,128)(2,1)} %protos_ref.3) | copy-start | bytes 1572868
  47.0 10.1 %copy-start.1 = (bf16[2,512]{1,0:T(2,128)(2,1)S(1)}, bf16[2,512]{1,0:T(2,128)(2,1)}, u32[]{:S(2)}) copy-start(bf16[2,512]{1,0:T(2,128)(2,1)} %student_ref.3) | copy-start | bytes 6148
